TPU v7x, 32 devices: a whole 2x2x4 slice. The times are simulated.
32 devices in a mesh: seq: 8 (over y, x, core), dp: 4 (over z).
Axes of the slice: x: 2, y: 2, z: 4, core: 2. Of those that a mesh axis runs over, the one named last changes fastest.
Arguments:
- queries: bfloat16 [8, 512, 4096], P('dp', 'seq'), may hold values from -8 to 8
- unrotated_key_rows: bfloat16 [8, 512, 1024], P('dp', 'seq'), may hold values from -8 to 8
- value_projection_rows: bfloat16 [8, 512, 1024], P('dp', 'seq'), may hold values from -6 to 6
- attention_output_gradient: bfloat16 [8, 512, 4096], P('dp', 'seq'), may hold values from -16 to 16
- normed_hidden_input: bfloat16 [8, 512, 4096], P('dp', 'seq'), may hold values from -6 to 6
- adapter_down_weight: bfloat16 [4096, 64], replicated, may hold values from -0.01171875 to 0.01171875
- adapter_up_weight: bfloat16 [64, 4096], replicated, may hold values from -0.01171875 to 0.01171875
- lengths: int32 [8], P('dp'), may hold values from 256 to 512, as said below
- offsets: int32 [8], P('dp'), may hold values from 0 to 31
Outputs:
- grad_query: bfloat16 [8, 512, 4096], P('dp', 'seq')
- grad_key: bfloat16 [8, 512, 1024], P('dp', 'seq')
- grad_value: bfloat16 [8, 512, 1024], P('dp', 'seq')
- grad_down: float32 [4096, 64], P('seq')
- grad_up: float32 [64, 4096], P(None, 'seq')
Inputs may be any that keep to these rules, and one draw needn't show every extreme that they name: `lengths`: in every draw at least one rollout has all 512 positions valid.
All inputs are finite; a program needn't handle non-finite values.
Results may differ from a plain program's by a relative error of at most 0.018.
The roundings to bfloat16 on the way count: a program that leaves them out, or rounds other values in their place, can miss the bound.
Values may be sent and summed in bfloat16 or wider, within the bound.
A program may use at most 64 MiB of HBM per device.

v0:
```python
from functools import partial
import jax
import jax.numpy as jnp
from jax import lax
from jax.sharding import PartitionSpec as P

HEAD_WIDTH = 128
rotary_base = 500000.0


def partner_2(value, axis, distance):
    mask = 2**distance
    pairs = [(source, source ^ mask) for source in range(lax.axis_size(axis))]
    return lax.ppermute(value, axis, pairs)


def rotary_tables(length, head_size):
    half_size = head_size // 2
    frequency = rotary_base ** (-(jnp.arange(half_size, dtype=jnp.float32) * 2.0 / head_size))
    angles = jnp.arange(length, dtype=jnp.float32)[:, None] * frequency[None, :]
    return (jnp.cos(angles), jnp.sin(angles))


def rotate(fields, cosine, sine_table, direction):
    half_size = fields.shape[-1] // 2
    first_half = fields[..., :half_size]
    second_half = fields[..., half_size:]
    cos_wide = cosine[:, None, :]
    sin_wide = direction * sine_table[:, None, :]
    return jnp.concatenate(
        [
            first_half * cos_wide - second_half * sin_wide,
            second_half * cos_wide + first_half * sin_wide,
        ],
        axis=-1,
    )


def contract_axes(first_operand, second_operand, first_axis, second_axis):
    return lax.dot_general(
        first_operand,
        second_operand,
        (((first_axis,), (second_axis,)), ((), ())),
        preferred_element_type=jnp.float32,
    )


def block_terms(rot_query, rot_key, value_head, grad_head, offset, begin_row, end_row, score_scale):
    row_index = jnp.arange(begin_row, end_row, dtype=jnp.int32)[:, None]
    col_index = jnp.arange(end_row, dtype=jnp.int32)[None, :]
    visible = (col_index == row_index) | (col_index >= offset) & (col_index <= row_index)
    query_block = rot_query[begin_row:end_row]
    grad_block = grad_head[begin_row:end_row]
    key_block = rot_key[:end_row]
    value_block = value_head[:end_row]
    scores = contract_axes(query_block, key_block, 1, 1) * score_scale
    row_max = jnp.max(jnp.where(visible, scores, -jnp.inf), axis=1, keepdims=True)
    row_total = jnp.sum(jnp.where(visible, jnp.exp(scores - row_max), 0.0), axis=1, keepdims=True)
    grad_prob = contract_axes(grad_block, value_block, 1, 1)
    probability = jnp.where(visible, jnp.exp(scores - row_max), 0.0) / row_total
    row_delta = jnp.sum(probability * grad_prob, axis=1, keepdims=True)
    prob_low = probability.astype(jnp.bfloat16)
    grad_score = (probability * (grad_prob - row_delta) * score_scale).astype(jnp.bfloat16)
    block_grad = jnp.dot(grad_score, key_block, preferred_element_type=jnp.float32)
    key_add = contract_axes(grad_score, query_block, 0, 0)
    value_add = contract_axes(prob_low, grad_block, 0, 0)
    return (block_grad, key_add, value_add)


def head_backward(rot_query, rot_key, value_head, grad_head, offset, block_rows):
    length = rot_query.shape[0]
    head_size = rot_query.shape[1]
    score_scale = head_size ** (-0.5)
    query_parts = []
    key_terms = []
    value_terms = []
    for block_index in range(length // block_rows):
        begin_row = block_index * block_rows
        end_row = begin_row + block_rows
        live_terms = partial(
            block_terms,
            rot_query,
            rot_key,
            value_head,
            grad_head,
            offset,
            begin_row,
            end_row,
            score_scale,
        )
        results = live_terms()
        block_grad, key_add, value_add = results
        query_parts.append(block_grad)
        key_terms.append(jnp.pad(key_add, ((0, length - end_row), (0, 0))))
        value_terms.append(jnp.pad(value_add, ((0, length - end_row), (0, 0))))
    key_accum = key_terms[0]
    value_accum = value_terms[0]
    for term_index in range(1, len(key_terms)):
        key_accum = key_accum + key_terms[term_index]
        value_accum = value_accum + value_terms[term_index]
    return (jnp.concatenate(query_parts, axis=0), key_accum, value_accum)


def arrange_rows(rows, share, part_rows, key_groups):
    rollout_count = rows.shape[0]
    split = rows.reshape(rollout_count, share, part_rows, key_groups, HEAD_WIDTH)
    return jnp.transpose(split, (0, 2, 3, 1, 4)).reshape(
        rollout_count, part_rows, key_groups * share, HEAD_WIDTH
    )


def join_group(paired, share, seq_parts, part_rows):
    my_index = lax.axis_index("seq")
    rollout_count = paired.shape[1]
    local_keys = paired.shape[3]
    joined = paired[None]
    for bit in range(share.bit_length() - 1):
        partner = partner_2(joined, "seq", bit)
        upper = my_index // (1 << bit) % 2
        joined = jnp.where(
            upper == 0,
            jnp.concatenate([joined, partner], axis=0),
            jnp.concatenate([partner, joined], axis=0),
        )
    ordered = joined.reshape(share, 2, rollout_count, seq_parts, part_rows, local_keys, HEAD_WIDTH)
    ordered = jnp.transpose(ordered, (1, 2, 3, 0, 4, 5, 6))
    return ordered.reshape(2, rollout_count, seq_parts * share * part_rows, local_keys, HEAD_WIDTH)


def reduce_group(partial_sums, share, seq_parts, part_rows):
    my_index = lax.axis_index("seq")
    rollout_count = partial_sums.shape[1]
    local_keys = partial_sums.shape[3]
    split = partial_sums.reshape(
        2, rollout_count, seq_parts, share, part_rows, local_keys, HEAD_WIDTH
    )
    split = jnp.transpose(split, (3, 0, 1, 2, 4, 5, 6))
    for bit in reversed(range(share.bit_length() - 1)):
        half = split.shape[0] // 2
        lower_half = split[:half]
        upper_half = split[half:]
        upper = my_index // (1 << bit) % 2
        keep = jnp.where(upper == 0, lower_half, upper_half)
        outgoing = jnp.where(upper == 0, upper_half, lower_half)
        split = keep + partner_2(outgoing.astype(jnp.bfloat16), "seq", bit).astype(outgoing.dtype)
    return split[0].reshape(2, rollout_count, seq_parts * part_rows, local_keys, HEAD_WIDTH)


def on_device(
    queries,
    unrotated_key_rows,
    value_projection_rows,
    attention_output_gradient,
    normed_hidden_input,
    adapter_down_weight,
    adapter_up_weight,
    lengths,
    offsets,
):
    rollout_count = queries.shape[0]
    tokens = queries.shape[1]
    seq_parts = lax.axis_size("seq")
    length = tokens * seq_parts
    query_width = queries.shape[2]
    head_count = query_width // HEAD_WIDTH
    key_groups = unrotated_key_rows.shape[2] // HEAD_WIDTH
    local_heads = head_count // seq_parts
    adapter_rank_size = adapter_down_weight.shape[1]
    share = max(1, seq_parts // key_groups)
    part_rows = tokens // share
    query_tokens = queries.reshape(rollout_count, tokens, head_count, HEAD_WIDTH)
    grad_tokens = attention_output_gradient.reshape(rollout_count, tokens, head_count, HEAD_WIDTH)
    key_arranged = arrange_rows(unrotated_key_rows, share, part_rows, key_groups)
    value_arranged = arrange_rows(value_projection_rows, share, part_rows, key_groups)
    query_heads, key_parted, value_parted, grad_heads = (
        lax.all_to_all(query_tokens, "seq", split_axis=2, concat_axis=1, tiled=True),
        lax.all_to_all(key_arranged, "seq", split_axis=2, concat_axis=1, tiled=True),
        lax.all_to_all(value_arranged, "seq", split_axis=2, concat_axis=1, tiled=True),
        lax.all_to_all(grad_tokens, "seq", split_axis=2, concat_axis=1, tiled=True),
    )
    paired = join_group(jnp.stack([key_parted, value_parted], axis=0), share, seq_parts, part_rows)
    key_heads = paired[0]
    value_heads = paired[1]
    local_keys = key_heads.shape[2]
    cosine, sine_table = rotary_tables(length, HEAD_WIDTH)
    positions = jnp.arange(length, dtype=jnp.int32)
    keep_mask = (positions[None, :] >= offsets[:, None]) & (positions[None, :] < lengths[:, None])
    grad_heads = jnp.where(keep_mask[:, :, None, None], grad_heads, jnp.zeros_like(grad_heads))
    rot_query = rotate(query_heads.astype(jnp.float32), cosine, sine_table, 1.0).astype(
        jnp.bfloat16
    )
    rot_key = rotate(key_heads.astype(jnp.float32), cosine, sine_table, 1.0).astype(jnp.bfloat16)
    block_rows = min(512, length)
    query_rolls = []
    key_rolls = []
    value_rolls = []
    for rollout_slot in range(rollout_count):
        query_list = []
        key_list = []
        value_list = []
        for head_slot in range(local_heads):
            key_slot = head_slot * local_keys // local_heads
            query_grad, key_grad, value_grad = head_backward(
                rot_query[rollout_slot, :, head_slot],
                rot_key[rollout_slot, :, key_slot],
                value_heads[rollout_slot, :, key_slot],
                grad_heads[rollout_slot, :, head_slot],
                offsets[rollout_slot],
                block_rows,
            )
            query_list.append(
                rotate(query_grad[:, None, :], cosine, sine_table, -1.0)[:, 0].astype(jnp.bfloat16)
            )
            key_list.append(
                rotate(key_grad[:, None, :], cosine, sine_table, -1.0)[:, 0].astype(jnp.bfloat16)
            )
            value_list.append(value_grad.astype(jnp.bfloat16))
        query_rolls.append(jnp.stack(query_list, axis=1))
        key_rolls.append(jnp.stack(key_list, axis=1))
        value_rolls.append(jnp.stack(value_list, axis=1))
    query_back = jnp.stack(query_rolls, axis=0)
    key_parts = jnp.stack(key_rolls, axis=0)
    value_parts = jnp.stack(value_rolls, axis=0)
    shared_heads = local_heads // local_keys
    key_local = (
        key_parts.astype(jnp.float32)
        .reshape(rollout_count, length, local_keys, shared_heads, HEAD_WIDTH)
        .sum(axis=3)
    )
    value_local = (
        value_parts.astype(jnp.float32)
        .reshape(rollout_count, length, local_keys, shared_heads, HEAD_WIDTH)
        .sum(axis=3)
    )
    summed = reduce_group(
        jnp.stack([key_local, value_local], axis=0), share, seq_parts, part_rows
    ).astype(jnp.bfloat16)
    query_result, key_result, value_result = (
        lax.all_to_all(query_back, "seq", split_axis=1, concat_axis=2, tiled=True),
        lax.all_to_all(summed[0], "seq", split_axis=1, concat_axis=2, tiled=True),
        lax.all_to_all(summed[1], "seq", split_axis=1, concat_axis=2, tiled=True),
    )
    key_total = jnp.transpose(
        key_result.reshape(rollout_count, part_rows, key_groups, share, HEAD_WIDTH), (0, 3, 1, 2, 4)
    ).reshape(rollout_count, tokens, key_groups * HEAD_WIDTH)
    value_total = jnp.transpose(
        value_result.reshape(rollout_count, part_rows, key_groups, share, HEAD_WIDTH),
        (0, 3, 1, 2, 4),
    ).reshape(rollout_count, tokens, key_groups * HEAD_WIDTH)
    flattened_query = query_result.reshape(rollout_count * tokens, query_width)
    hidden_state = normed_hidden_input.reshape(rollout_count * tokens, normed_hidden_input.shape[2])
    adapter_latent = jnp.dot(
        hidden_state, adapter_down_weight, preferred_element_type=jnp.float32
    ).astype(jnp.bfloat16)
    backward_gradient = contract_axes(flattened_query, adapter_up_weight, 1, 1).astype(jnp.bfloat16)
    joined_terms = lax.psum_scatter(
        jnp.concatenate(
            [
                contract_axes(hidden_state, backward_gradient, 0, 0),
                contract_axes(flattened_query, adapter_latent, 0, 0),
            ],
            axis=1,
        ).astype(jnp.bfloat16),
        "seq",
        scatter_dimension=0,
        tiled=True,
    ).astype(jnp.float32)
    down_local = joined_terms[:, :adapter_rank_size]
    up_local = joined_terms[:, adapter_rank_size:]
    down_sum, up_sum = (
        lax.psum(down_local.astype(jnp.bfloat16), "dp").astype(jnp.float32),
        lax.psum(up_local.astype(jnp.bfloat16), "dp").astype(jnp.float32),
    )
    return (
        flattened_query.reshape(rollout_count, tokens, query_width),
        key_total,
        value_total,
        down_sum,
        up_sum.T,
    )


def solution(mesh):
    in_specs = (
        P("dp", "seq", None),
        P("dp", "seq", None),
        P("dp", "seq", None),
        P("dp", "seq", None),
        P("dp", "seq", None),
        P(),
        P(),
        P("dp"),
        P("dp"),
    )
    out_specs = (
        P("dp", "seq", None),
        P("dp", "seq", None),
        P("dp", "seq", None),
        P("seq", None),
        P(None, "seq"),
    )
    return jax.shard_map(
        on_device, mesh=mesh, in_specs=in_specs, out_specs=out_specs, check_vma=False
    )
```

profile of v0, /device:TPU:0, one launch (start us, length us, event | category | flops | bytes accessed | tf_op | source)
XLA Modules:
  0.0 218.1 jit_solution(3533386464252049813)
XLA Ops:
  7.2 1.9 copy_bitcast_fusion.3
  9.1 5.2 %all-to-all-start.1 = ((bf16[2,64,8,128]{3,1,0,2:T(8,128)(2,1)}), bf16[2,64,8,128]{3,1,0,2:T(8,128)(2,1)S(1)}, u32[]{:S(2)}, u32[]{:S(2)}) async-start(bf16[2,64,8,128]{3,1,0,2:T(8,128)(2,1)} %copy_bitcast_fusion.3), calls=%async_computation.1 | async-start | bytes 524288 | tf_op jit(solution)/shard_map/all_to_all | solution.py:177
  14.3 1.3 fusion.96
  15.6 1.0 fusion.38
  16.6 1.3 copy_bitcast_fusion.1
  17.9 1.3 copy_bitcast_fusion
  19.2 0.8 copy_bitcast_fusion.2
  20.0 1.2 all-to-all-done.1
  21.2 3.4 %all-to-all-start.3 = ((bf16[2,64,8,128]{3,1,0,2:T(8,128)(2,1)}), bf16[2,64,8,128]{3,1,0,2:T(8,128)(2,1)S(1)}, u32[]{:S(2)}, u32[]{:S(2)}) async-start(bf16[2,64,8,128]{3,1,0,2:T(8,128)(2,1)} %copy_bitcast_fusion.2), calls=%async_computation.3 | async-start | bytes 524288 | tf_op jit(solution)/shard_map/all_to_all | solution.py:178
  24.6 0.7 iota_compare_fusion.3
  25.3 6.1 %all-to-all-done.3 = bf16[2,64,8,128]{3,1,0,2:T(8,128)(2,1)S(1)} async-done(((bf16[2,64,8,128]{3,1,0,2:T(8,128)(2,1)}), bf16[2,64,8,128]{3,1,0,2:T(8,128)(2,1)S(1)}, u32[]{:S(2)}, u32[]{:S(2)}) %all-to-all-start.3) | async-done | bytes 262176 | tf_op jit(solution)/shard_map/all_to_all | solution.py:178
  31.4 3.6 %all-to-all-start = ((bf16[2,64,32,128]{3,1,0,2:T(8,128)(2,1)}), bf16[2,64,32,128]{3,1,0,2:T(8,128)(2,1)S(1)}, u32[]{:S(2)}, u32[]{:S(2)}) async-start(bf16[2,64,32,128]{3,1,0,2:T(8,128)(2,1)} %copy_bitcast_fusion.1), calls=%async_computation | async-start | bytes 2097152 | tf_op jit(solution)/shard_map/all_to_all | solution.py:176
  36.2 0.7 fusion.95
  36.9 13.4 %all-to-all-done = bf16[2,64,32,128]{3,1,0,2:T(8,128)(2,1)S(1)} async-done(((bf16[2,64,32,128]{3,1,0,2:T(8,128)(2,1)}), bf16[2,64,32,128]{3,1,0,2:T(8,128)(2,1)S(1)}, u32[]{:S(2)}, u32[]{:S(2)}) %all-to-all-start) | async-done | bytes 1048608 | tf_op jit(solution)/shard_map/all_to_all | solution.py:176
  50.3 4.4 %all-to-all-start.2 = ((bf16[2,64,32,128]{3,1,0,2:T(8,128)(2,1)}), bf16[2,64,32,128]{3,1,0,2:T(8,128)(2,1)}, u32[]{:S(2)}, u32[]{:S(2)}) async-start(bf16[2,64,32,128]{3,1,0,2:T(8,128)(2,1)} %copy_bitcast_fusion), calls=%async_computation.2 | async-start | bytes 2097152 | tf_op jit(solution)/shard_map/all_to_all | solution.py:179
  55.2 0.8 copy-done.25
  56.1 0.8 add_convert_fusion
  56.9 1.3 convolution_multiply_fusion.6
  58.2 1.3 convolution_multiply_fusion.5
  59.6 1.4 convolution_multiply_fusion.4
  61.1 1.3 convolution_multiply_fusion.2
  62.4 1.4 convolution_multiply_fusion.1
  63.8 1.3 convolution_multiply_fusion
  65.1 4.9 %all-to-all-done.2 = bf16[2,64,32,128]{3,1,0,2:T(8,128)(2,1)} async-done(((bf16[2,64,32,128]{3,1,0,2:T(8,128)(2,1)}), bf16[2,64,32,128]{3,1,0,2:T(8,128)(2,1)}, u32[]{:S(2)}, u32[]{:S(2)}) %all-to-all-start.2) | async-done | bytes 1048608 | tf_op jit(solution)/shard_map/all_to_all | solution.py:179
  69.9 1.3 copy.65
  73.1 1.0 fusion.1
  74.8 1.0 fusion.5
  77.5 1.0 fusion.6
  79.2 1.0 fusion.7
  80.2 1.0 fusion.8
  81.8 0.9 multiply_convert_fusion.3
  87.2 0.8 multiply_reduce_fusion.5
  88.0 0.9 multiply_convert_fusion.7
  90.5 0.7 subtract_convert_fusion.17
  91.1 0.7 subtract_convert_fusion.16
  91.9 1.1 pad_maximum_fusion
  93.0 2.4 %copy.68 = bf16[2,512,4,128]{3,2,0,1:T(4,128)(2,1)} copy(bf16[2,512,4,128]{1,3,2,0:T(8,128)(2,1)} %pad_maximum_fusion) | data formatting | bytes 2097152 | tf_op jit(solution)/shard_map/stack | solution.py:221
  95.4 4.2 %all-to-all-start.4 = ((bf16[2,512,4,128]{3,2,0,1:T(4,128)(2,1)}), bf16[2,512,4,128]{3,2,0,1:T(4,128)(2,1)}, u32[]{:S(2)}, u32[]{:S(2)}) async-start(bf16[2,512,4,128]{3,2,0,1:T(4,128)(2,1)} %copy.68), calls=%async_computation.4 | async-start | bytes 2097152 | tf_op jit(solution)/shard_map/all_to_all | solution.py:239
  99.7 1.7 fusion.3
  101.5 1.4 fusion.4
  103.2 1.0 copy.74
  104.2 1.1 convolution_bitcast_fusion.3
  105.3 1.1 convolution_bitcast_fusion.2
  106.3 8.7 %all-to-all-done.4 = bf16[2,512,4,128]{3,2,0,1:T(4,128)(2,1)} async-done(((bf16[2,512,4,128]{3,2,0,1:T(4,128)(2,1)}), bf16[2,512,4,128]{3,2,0,1:T(4,128)(2,1)}, u32[]{:S(2)}, u32[]{:S(2)}) %all-to-all-start.4) | async-done | bytes 1048608 | tf_op jit(solution)/shard_map/all_to_all | solution.py:239
  115.1 3.4 %all-to-all-start.6 = ((bf16[2,512,1,128]{3,0,2,1:T(2,128)(2,1)}), bf16[2,512,1,128]{3,0,2,1:T(2,128)(2,1)S(1)}, u32[]{:S(2)}, u32[]{:S(2)}) async-start(bf16[2,512,1,128]{3,0,2,1:T(2,128)(2,1)} %copy.74), calls=%async_computation.6 | async-start | bytes 524288 | tf_op jit(solution)/shard_map/all_to_all | solution.py:241
  118.5 1.4 copy.69
  119.9 1.8 copy.70
  121.7 2.6 %reshape.691 = bf16[128,4096]{1,0:T(8,128)(2,1)} reshape(bf16[2,64,8,4,128]{4,3,2,1,0:T(4,128)(2,1)} %copy.70) | data formatting | bytes 2097152 | tf_op jit(solution)/shard_map/reshape | solution.py:250
  124.3 3.2 %convolution_convert_fusion = bf16[4096,64]{0,1:T(8,128)(2,1)} fusion(bf16[128,4096]{1,0:T(8,128)(2,1)} %reshape.691, bf16[128,4096]{1,0:T(8,128)(2,1)S(1)} %bitcast.267, bf16[4096,64]{0,1:T(8,128)(2,1)} %param.14), kind=kOutput, calls=%fused_computation | convolution fusion | flops 134488064 | bytes 3145728 | tf_op jit(solution)/shard_map/dot_general | solution.py:40
  127.4 3.1 %fusion = bf16[4096,64]{0,1:T(8,128)(2,1)} fusion(bf16[128,4096]{1,0:T(8,128)(2,1)S(1)} %bitcast.266, bf16[128,4096]{1,0:T(8,128)(2,1)} %reshape.691, bf16[64,4096]{1,0:T(8,128)(2,1)} %param.15), kind=kOutput, calls=%fused_computation.2 | convolution fusion | flops 134488064 | bytes 3145728 | tf_op jit(solution)/shard_map/dot_general | solution.py:40
  130.5 2.3 %pad_maximum_fusion.1 = bf16[4096,128]{0,1:T(8,128)(2,1)} fusion(bf16[4096,64]{0,1:T(8,128)(2,1)} %convolution_convert_fusion, bf16[4096,64]{0,1:T(8,128)(2,1)} %fusion), kind=kLoop, calls=%fused_computation.53 | loop fusion | flops 2097152 | bytes 2097152 | tf_op jit(solution)/shard_map/concatenate | solution.py:257
  132.8 1.5 convolution_bitcast_fusion.1
  138.8 0.7 subtract_convert_fusion.9
  139.5 0.7 subtract_convert_fusion.8
  140.6 0.9 copy.71
  141.5 4.2 %all-to-all-start.5 = ((bf16[2,512,1,128]{3,0,2,1:T(2,128)(2,1)}), bf16[2,512,1,128]{3,0,2,1:T(2,128)(2,1)S(1)}, u32[]{:S(2)}, u32[]{:S(2)}) async-start(bf16[2,512,1,128]{3,0,2,1:T(2,128)(2,1)} %copy.71), calls=%async_computation.5 | async-start | bytes 524288 | tf_op jit(solution)/shard_map/all_to_all | solution.py:240
  145.7 24.8 %reduce-scatter.2.cloned.1.call-done = bf16[512,128]{0,1:T(8,128)(2,1)} async-done(((bf16[4096,128]{0,1:T(8,128)(2,1)}), bf16[512,128]{0,1:T(8,128)(2,1)}) %reduce-scatter.2.cloned.1.call-update) | async-done | bytes 131088 | tf_op jit(solution)/shard_map/reduce_scatter | solution.py:256
  170.5 1.5 slice_bitcast_fusion.24
  172.3 0.8 reshape_transpose_reshape.15
  173.4 0.8 reshape_transpose_reshape.14
  174.2 1.6 reshape_reshape.3
  175.8 32.4 %all-reduce.3.cloned.1.call-done = (bf16[512,64]{0,1:T(8,128)(2,1)}, bf16[64,512]{1,0:T(8,128)(2,1)}) async-done(((bf16[512,64]{0,1:T(8,128)(2,1)}, bf16[64,512]{1,0:T(8,128)(2,1)}), (bf16[512,64]{0,1:T(8,128)(2,1)}, bf16[64,512]{1,0:T(8,128)(2,1)})) %all-reduce.3.cloned.1.call-update) | async-done | bytes 131088 | tf_op jit(solution)/shard_map/psum | solution.py:271
  208.2 1.5 convert_element_type.321
  209.7 1.5 transpose.52
  (149 shorter events, 18.8 us)
Async XLA Ops:
  7.2 117.1 %copy-start = (bf16[2,64,4096]{2,1,0:T(8,128)(2,1)S(1)}, bf16[2,64,4096]{2,1,0:T(8,128)(2,1)}, u32[]{:S(2)}) copy-start(bf16[2,64,4096]{2,1,0:T(8,128)(2,1)} %param.13) | copy-start | bytes 3145732
  7.2 9.4 %copy-start.29 = (bf16[2,64,4096]{2,1,0:T(8,128)(2,1)S(1)}, bf16[2,64,4096]{2,1,0:T(8,128)(2,1)}, u32[]{:S(2)}) copy-start(bf16[2,64,4096]{2,1,0:T(8,128)(2,1)} %param.9) | copy-start | bytes 3145732
  9.1 12.1 %all-to-all-start.1 = ((bf16[2,64,8,128]{3,1,0,2:T(8,128)(2,1)}), bf16[2,64,8,128]{3,1,0,2:T(8,128)(2,1)S(1)}, u32[]{:S(2)}, u32[]{:S(2)}) async-start(bf16[2,64,8,128]{3,1,0,2:T(8,128)(2,1)} %copy_bitcast_fusion.3), calls=%async_computation.1 | async-start | bytes 524288 | tf_op jit(solution)/shard_map/all_to_all | solution.py:177
  14.3 3.7 %copy-start.30 = (bf16[2,64,4096]{2,1,0:T(8,128)(2,1)S(1)}, bf16[2,64,4096]{2,1,0:T(8,128)(2,1)}, u32[]{:S(2)}) copy-start(bf16[2,64,4096]{2,1,0:T(8,128)(2,1)} %param.12) | copy-start | bytes 3145732
  16.6 19.1 %copy-start.24 = (f32[512,64]{1,0:T(8,128)}, f32[512,64]{1,0:T(8,128)S(1)}, u32[]{:S(2)}) copy-start(f32[512,64]{1,0:T(8,128)S(1)} %get-tuple-element.99) | copy-start | bytes 393220
  16.6 19.1 %copy-start.26 = (f32[512,64]{1,0:T(8,128)}, f32[512,64]{1,0:T(8,128)S(1)}, u32[]{:S(2)}) copy-start(f32[512,64]{1,0:T(8,128)S(1)} %get-tuple-element.100) | copy-start | bytes 393220
  16.6 2.6 %copy-start.35 = (bf16[2,64,1024]{2,1,0:T(8,128)(2,1)S(1)}, bf16[2,64,1024]{2,1,0:T(8,128)(2,1)}, u32[]{:S(2)}) copy-start(bf16[2,64,1024]{2,1,0:T(8,128)(2,1)} %param.11) | copy-start | bytes 786436
  17.9 7.3 %copy-start.41 = (s32[2]{0:T(128)S(1)}, s32[2]{0:T(128)}, u32[]{:S(2)}) copy-start(s32[2]{0:T(128)} %param.17) | copy-start | bytes 28
  17.9 7.3 %copy-start.46 = (s32[2]{0:T(128)S(1)}, s32[2]{0:T(128)}, u32[]{:S(2)}) copy-start(s32[2]{0:T(128)} %param.16) | copy-start | bytes 28
  21.2 10.3 %all-to-all-start.3 = ((bf16[2,64,8,128]{3,1,0,2:T(8,128)(2,1)}), bf16[2,64,8,128]{3,1,0,2:T(8,128)(2,1)S(1)}, u32[]{:S(2)}, u32[]{:S(2)}) async-start(bf16[2,64,8,128]{3,1,0,2:T(8,128)(2,1)} %copy_bitcast_fusion.2), calls=%async_computation.3 | async-start | bytes 524288 | tf_op jit(solution)/shard_map/all_to_all | solution.py:178
  31.4 18.9 %all-to-all-start = ((bf16[2,64,32,128]{3,1,0,2:T(8,128)(2,1)}), bf16[2,64,32,128]{3,1,0,2:T(8,128)(2,1)S(1)}, u32[]{:S(2)}, u32[]{:S(2)}) async-start(bf16[2,64,32,128]{3,1,0,2:T(8,128)(2,1)} %copy_bitcast_fusion.1), calls=%async_computation | async-start | bytes 2097152 | tf_op jit(solution)/shard_map/all_to_all | solution.py:176
  50.3 19.6 %all-to-all-start.2 = ((bf16[2,64,32,128]{3,1,0,2:T(8,128)(2,1)}), bf16[2,64,32,128]{3,1,0,2:T(8,128)(2,1)}, u32[]{:S(2)}, u32[]{:S(2)}) async-start(bf16[2,64,32,128]{3,1,0,2:T(8,128)(2,1)} %copy_bitcast_fusion), calls=%async_computation.2 | async-start | bytes 2097152 | tf_op jit(solution)/shard_map/all_to_all | solution.py:179
  55.1 1.0 copy-start.25
  55.1 1.0 copy-start.27
  69.9 1.6 copy-start.34
  71.3 0.9 copy-start.33
  71.5 15.6 %copy-start.28 = (bf16[2,512,4,128]{3,1,2,0:T(8,128)(2,1)}, bf16[2,512,4,128]{3,1,2,0:T(8,128)(2,1)S(1)}, u32[]{:S(2)}) copy-start(bf16[2,512,4,128]{3,1,2,0:T(8,128)(2,1)S(1)} %bitcast_select_fusion) | copy-start | bytes 3145732
  74.8 1.2 copy-start.2
  74.8 1.6 copy-start.22
  74.8 1.9 copy-start.23
  82.7 1.2 copy-start.4
  82.7 1.2 copy-start.7
  82.7 1.2 copy-start.9
  83.3 1.2 copy-start.1
  83.3 1.5 copy-start.19
  83.3 2.0 copy-start.21
  84.0 1.9 copy-start.6
  87.1 0.8 copy-start.42
  87.2 2.3 %copy-start.44 = (f32[512]{0:T(512)}, f32[512]{0:T(512)S(1)}, u32[]{:S(2)}) copy-start(f32[512]{0:T(512)S(1)} %get-tuple-element.10) | copy-start | bytes 6148
  88.9 0.9 copy-start.13
  88.9 1.0 copy-start.15
  88.9 1.3 copy-start.11
  89.9 1.9 copy-start.17
  93.0 6.7 %copy-start.45 = (f32[512]{0:T(512)S(1)}, f32[512]{0:T(512)}, u32[]{:S(2)}) copy-start(f32[512]{0:T(512)} %copy-done.44) | copy-start | bytes 6148
  95.4 19.6 %all-to-all-start.4 = ((bf16[2,512,4,128]{3,2,0,1:T(4,128)(2,1)}), bf16[2,512,4,128]{3,2,0,1:T(4,128)(2,1)}, u32[]{:S(2)}, u32[]{:S(2)}) async-start(bf16[2,512,4,128]{3,2,0,1:T(4,128)(2,1)} %copy.68), calls=%async_computation.4 | async-start | bytes 2097152 | tf_op jit(solution)/shard_map/all_to_all | solution.py:239
  99.7 1.7 copy-start.20
  99.7 1.7 copy-start.43
  101.4 1.4 copy-start.36
  101.4 1.4 copy-start.37
  101.4 1.4 copy-start.38
  101.4 1.4 copy-start.39
  101.4 1.4 copy-start.40
  102.9 1.3 copy-start.10
  103.0 2.2 %copy-start.8 = (bf16[512,512]{0,1:T(8,128)(2,1)S(1)}, bf16[512,512]{0,1:T(8,128)(2,1)}, u32[]{:S(2)}) copy-start(bf16[512,512]{0,1:T(8,128)(2,1)} %copy-done.7) | copy-start | bytes 1572868
  115.1 26.4 %all-to-all-start.6 = ((bf16[2,512,1,128]{3,0,2,1:T(2,128)(2,1)}), bf16[2,512,1,128]{3,0,2,1:T(2,128)(2,1)S(1)}, u32[]{:S(2)}, u32[]{:S(2)}) async-start(bf16[2,512,1,128]{3,0,2,1:T(2,128)(2,1)} %copy.74), calls=%async_computation.6 | async-start | bytes 524288 | tf_op jit(solution)/shard_map/all_to_all | solution.py:241
  118.5 52.1 %reduce-scatter.2.cloned.1.call-start = ((), (), s32[]{:S(2)}) async-start(), calls=%async_computation.8 | async-start | bytes 1179648 | tf_op jit(solution)/shard_map/reduce_scatter | solution.py:256
  132.8 1.5 copy-start.16
  134.3 1.0 copy-start.14
  135.4 1.0 copy-start.12
  136.4 1.0 copy-start.18
  137.4 1.0 copy-start.5
  137.4 1.4 copy-start.32
  137.5 2.0 copy-start.31
  141.4 32.7 %copy-start.3 = (bf16[2,64,8,4,128]{4,3,2,1,0:T(4,128)(2,1)S(1)}, bf16[2,64,8,4,128]{4,3,2,1,0:T(4,128)(2,1)}, u32[]{:S(2)}) copy-start(bf16[2,64,8,4,128]{4,3,2,1,0:T(4,128)(2,1)} %copy.70) | copy-start | bytes 3145732
  141.5 31.7 %all-to-all-start.5 = ((bf16[2,512,1,128]{3,0,2,1:T(2,128)(2,1)}), bf16[2,512,1,128]{3,0,2,1:T(2,128)(2,1)S(1)}, u32[]{:S(2)}, u32[]{:S(2)}) async-start(bf16[2,512,1,128]{3,0,2,1:T(2,128)(2,1)} %copy.71), calls=%async_computation.5 | async-start | bytes 524288 | tf_op jit(solution)/shard_map/all_to_all | solution.py:240
  145.7 62.5 %all-reduce.3.cloned.1.call-start = ((), (), s32[]{:S(2)}) async-start(), calls=%async_computation.9 | async-start | bytes 262144 | tf_op jit(solution)/shard_map/psum | solution.py:271
Sparse Core Ops, SparseCore 0:
  132.9 37.5 reduce-scatter.1
  173.5 34.6 all-reduce.2
where the time goes:
time: 219 us; the launch traced here: 218 us
  waiting for transfers between devices  91.6 us (42%)
  matrix products  35.7 us (16%)
  local copies, waits for them, and re-layouts  30 us (14%)
  starting transfers between devices  28.5 us (13%)
  other arithmetic  17.3 us (8%)
  between operations  14.9 us (7%)
    dot_general x34, matrix products, contract_axes(): lax.dot_general(first_operand, second_operand, (((first_axis,), (second_a...  33.6 us
    psum x1, waiting for transfers between devices, on_device(): lax.psum(down_local.astype(jnp.bfloat16), 'dp').astype(jnp.float32)  32.4 us
    reduce_scatter x1, waiting for transfers between devices, on_device(): lax.psum_scatter(jnp.concatenate([contract_axes(hidden_state, backward_gr...  24.8 us
    all_to_all x1, waiting for transfers between devices, on_device(): lax.all_to_all(query_tokens, 'seq', split_axis=2, concat_axis=1, tiled=True)  13.4 us
    all_to_all x1, waiting for transfers between devices, on_device(): lax.all_to_all(query_back, 'seq', split_axis=1, concat_axis=2, tiled=True)  8.72 us
    all_to_all x1, waiting for transfers between devices, on_device(): lax.all_to_all(value_arranged, 'seq', split_axis=2, concat_axis=1, tiled=...  6.08 us
    unnamed x94, local copies, waits for them, and re-layouts  5.95 us
    all_to_all x1, starting transfers between devices, on_device(): lax.all_to_all(key_arranged, 'seq', split_axis=2, concat_axis=1, tiled=True)  5.2 us
  transfers between devices with their start and end apart: 9, of which 7 were waited for; matrix products, arithmetic and copies ran while one was open for 23% of the time, Pallas kernels for 0%

commit v1 on v0

--- a/solution.py
+++ b/solution.py
@@ -173,7 +173,12 @@
     key_arranged = arrange_rows(unrotated_key_rows, share, part_rows, key_groups)
     value_arranged = arrange_rows(value_projection_rows, share, part_rows, key_groups)
     query_heads, key_parted, value_parted, grad_heads = (
-        lax.all_to_all(query_tokens, "seq", split_axis=2, concat_axis=1, tiled=True),
+        jnp.concatenate(
+            lax.all_to_all(
+                jnp.stack(jnp.split(query_tokens, lax.axis_size("seq"), axis=2)), "seq", 0, 0
+            ),
+            axis=1,
+        ),
         lax.all_to_all(key_arranged, "seq", split_axis=2, concat_axis=1, tiled=True),
         lax.all_to_all(value_arranged, "seq", split_axis=2, concat_axis=1, tiled=True),
         lax.all_to_all(grad_tokens, "seq", split_axis=2, concat_axis=1, tiled=True),

time: 219 us -> 228 us (1.041)
  local copies, waits for them, and re-layouts: 30 us -> 39.4 us
  waiting for transfers between devices: 91.6 us -> 88.4 us
    unnamed x94 -> x98, local copies, waits for them, and re-layouts: 5.95 us -> 14.1 us
  transfers between devices with their start and end apart: 9 -> 9, of which waited for: 7 -> 6; matrix products, arithmetic and copies ran while one was open for 23% -> 26% of each run, Pallas kernels for 0% -> 0%
where the time goes in v1:
time: 228 us; the launch traced here: 227 us
  waiting for transfers between devices  88.4 us (39%)
  local copies, waits for them, and re-layouts  39.4 us (17%)
  matrix products  35.7 us (16%)
  starting transfers between devices  29.3 us (13%)
  other arithmetic  19.2 us (8%)
  between operations  14.9 us (7%)
    dot_general x34, matrix products, contract_axes(): lax.dot_general(first_operand, second_operand, (((first_axis,), (second_a...  33.6 us
    psum x1, waiting for transfers between devices, on_device(): lax.psum(down_local.astype(jnp.bfloat16), 'dp').astype(jnp.float32)  32.4 us
    reduce_scatter x1, waiting for transfers between devices, on_device(): lax.psum_scatter(jnp.concatenate([contract_axes(hidden_state, backward_gr...  24.8 us
    unnamed x98, local copies, waits for them, and re-layouts  14.1 us
    all_to_all x1, waiting for transfers between devices, on_device(): lax.all_to_all(jnp.stack(jnp.split(query_tokens, lax.axis_size('seq'), ax...  12.5 us
    all_to_all x1, waiting for transfers between devices, on_device(): lax.all_to_all(query_back, 'seq', split_axis=1, concat_axis=2, tiled=True)  8.72 us
    all_to_all x1, waiting for transfers between devices, on_device(): lax.all_to_all(value_arranged, 'seq', split_axis=2, concat_axis=1, tiled=...  6.18 us
    all_to_all x1, starting transfers between devices, on_device(): lax.all_to_all(key_arranged, 'seq', split_axis=2, concat_axis=1, tiled=True)  5.2 us
  transfers between devices with their start and end apart: 9, of which 6 were waited for; matrix products, arithmetic and copies ran while one was open for 26% of the time, Pallas kernels for 0%

profile of v1, /device:TPU:0, one launch (start us, length us, event | category | flops | bytes accessed | tf_op | source)
XLA Modules:
  0.0 227.0 jit_solution(6151959438260258685)
XLA Ops:
  7.2 1.8 copy_bitcast_fusion.2
  9.0 5.2 %all-to-all-start.1 = ((bf16[2,64,8,128]{3,1,0,2:T(8,128)(2,1)}), bf16[2,64,8,128]{3,1,0,2:T(8,128)(2,1)S(1)}, u32[]{:S(2)}, u32[]{:S(2)}) async-start(bf16[2,64,8,128]{3,1,0,2:T(8,128)(2,1)} %copy_bitcast_fusion.2), calls=%async_computation.1 | async-start | bytes 524288 | tf_op jit(solution)/shard_map/all_to_all | solution.py:182
  14.2 1.3 fusion.104
  16.2 0.7 compare_and_fusion
  16.9 1.7 copy_bitcast_fusion.1
  18.6 1.0 fusion.38
  19.6 1.6 copy.84
  22.0 0.7 fusion.56
  23.4 0.7 fusion.54
  24.8 0.7 fusion.52
  25.5 1.3 copy_bitcast_fusion
  27.5 4.2 %all-to-all-start.3 = ((bf16[2,64,8,128]{3,1,0,2:T(8,128)(2,1)}), bf16[2,64,8,128]{3,1,0,2:T(8,128)(2,1)S(1)}, u32[]{:S(2)}, u32[]{:S(2)}) async-start(bf16[2,64,8,128]{3,1,0,2:T(8,128)(2,1)} %copy_bitcast_fusion.1), calls=%async_computation.3 | async-start | bytes 524288 | tf_op jit(solution)/shard_map/all_to_all | solution.py:183
  31.7 0.7 fusion.50
  32.5 6.2 %all-to-all-done.3 = bf16[2,64,8,128]{3,1,0,2:T(8,128)(2,1)S(1)} async-done(((bf16[2,64,8,128]{3,1,0,2:T(8,128)(2,1)}), bf16[2,64,8,128]{3,1,0,2:T(8,128)(2,1)S(1)}, u32[]{:S(2)}, u32[]{:S(2)}) %all-to-all-start.3) | async-done | bytes 262176 | tf_op jit(solution)/shard_map/all_to_all | solution.py:183
  39.3 3.6 %all-to-all-start = ((bf16[8,2,64,4,128]{4,3,2,1,0:T(4,128)(2,1)}), bf16[8,2,64,4,128]{4,3,2,1,0:T(4,128)(2,1)S(1)}, u32[]{:S(2)}, u32[]{:S(2)}) async-start(bf16[8,2,64,4,128]{4,3,2,1,0:T(4,128)(2,1)} %fusion.50), calls=%async_computation | async-start | bytes 2097152 | tf_op jit(solution)/shard_map/all_to_all | solution.py:177
  43.6 1.0 copy.90
  45.7 12.5 %all-to-all-done = bf16[8,2,64,4,128]{4,3,2,1,0:T(4,128)(2,1)S(1)} async-done(((bf16[8,2,64,4,128]{4,3,2,1,0:T(4,128)(2,1)}), bf16[8,2,64,4,128]{4,3,2,1,0:T(4,128)(2,1)S(1)}, u32[]{:S(2)}, u32[]{:S(2)}) %all-to-all-start) | async-done | bytes 1048608 | tf_op jit(solution)/shard_map/all_to_all | solution.py:177
  58.2 1.0 copy-done.24
  59.2 4.4 %all-to-all-start.2 = ((bf16[2,64,32,128]{3,1,0,2:T(8,128)(2,1)}), bf16[2,64,32,128]{3,1,0,2:T(8,128)(2,1)}, u32[]{:S(2)}, u32[]{:S(2)}) async-start(bf16[2,64,32,128]{3,1,0,2:T(8,128)(2,1)} %copy_bitcast_fusion), calls=%async_computation.2 | async-start | bytes 2097152 | tf_op jit(solution)/shard_map/all_to_all | solution.py:184
  63.6 1.4 convert_bitcast_fusion
  66.1 0.8 add_convert_fusion
  66.9 1.3 convolution_multiply_fusion.6
  68.2 1.3 convolution_multiply_fusion.5
  69.6 1.4 convolution_multiply_fusion.4
  71.1 1.3 convolution_multiply_fusion.2
  72.4 1.4 convolution_multiply_fusion.1
  73.8 1.3 convolution_multiply_fusion
  75.1 3.7 %all-to-all-done.2 = bf16[2,64,32,128]{3,1,0,2:T(8,128)(2,1)} async-done(((bf16[2,64,32,128]{3,1,0,2:T(8,128)(2,1)}), bf16[2,64,32,128]{3,1,0,2:T(8,128)(2,1)}, u32[]{:S(2)}, u32[]{:S(2)}) %all-to-all-start.2) | async-done | bytes 1048608 | tf_op jit(solution)/shard_map/all_to_all | solution.py:184
  78.8 1.3 copy.67
  82.0 1.0 fusion.1
  83.7 1.0 fusion.5
  86.4 1.0 fusion.6
  88.1 1.0 fusion.7
  89.1 1.0 fusion.8
  90.7 0.9 multiply_convert_fusion.3
  96.1 0.8 multiply_reduce_fusion.5
  96.9 0.9 multiply_convert_fusion.7
  100.8 1.1 pad_maximum_fusion
  101.9 2.4 %copy.70 = bf16[2,512,4,128]{3,2,0,1:T(4,128)(2,1)} copy(bf16[2,512,4,128]{1,3,2,0:T(8,128)(2,1)} %pad_maximum_fusion) | data formatting | bytes 2097152 | tf_op jit(solution)/shard_map/stack | solution.py:226
  104.3 4.2 %all-to-all-start.4 = ((bf16[2,512,4,128]{3,2,0,1:T(4,128)(2,1)}), bf16[2,512,4,128]{3,2,0,1:T(4,128)(2,1)}, u32[]{:S(2)}, u32[]{:S(2)}) async-start(bf16[2,512,4,128]{3,2,0,1:T(4,128)(2,1)} %copy.70), calls=%async_computation.4 | async-start | bytes 2097152 | tf_op jit(solution)/shard_map/all_to_all | solution.py:244
  108.6 1.7 fusion.3
  110.4 1.4 fusion.4
  112.1 1.0 copy.76
  113.0 1.1 convolution_bitcast_fusion.3
  114.1 1.1 convolution_bitcast_fusion.2
  115.2 8.7 %all-to-all-done.4 = bf16[2,512,4,128]{3,2,0,1:T(4,128)(2,1)} async-done(((bf16[2,512,4,128]{3,2,0,1:T(4,128)(2,1)}), bf16[2,512,4,128]{3,2,0,1:T(4,128)(2,1)}, u32[]{:S(2)}, u32[]{:S(2)}) %all-to-all-start.4) | async-done | bytes 1048608 | tf_op jit(solution)/shard_map/all_to_all | solution.py:244
  123.9 3.4 %all-to-all-start.6 = ((bf16[2,512,1,128]{3,0,2,1:T(2,128)(2,1)}), bf16[2,512,1,128]{3,0,2,1:T(2,128)(2,1)S(1)}, u32[]{:S(2)}, u32[]{:S(2)}) async-start(bf16[2,512,1,128]{3,0,2,1:T(2,128)(2,1)} %copy.76), calls=%async_computation.6 | async-start | bytes 524288 | tf_op jit(solution)/shard_map/all_to_all | solution.py:246
  127.4 1.4 copy.71
  128.8 1.8 copy.72
  130.6 2.6 %reshape.691 = bf16[128,4096]{1,0:T(8,128)(2,1)} reshape(bf16[2,64,8,4,128]{4,3,2,1,0:T(4,128)(2,1)} %copy.72) | data formatting | bytes 2097152 | tf_op jit(solution)/shard_map/reshape | solution.py:255
  133.2 3.2 %convolution_convert_fusion = bf16[4096,64]{0,1:T(8,128)(2,1)} fusion(bf16[128,4096]{1,0:T(8,128)(2,1)} %reshape.691, bf16[128,4096]{1,0:T(8,128)(2,1)S(1)} %bitcast.296, bf16[4096,64]{0,1:T(8,128)(2,1)} %param.14), kind=kOutput, calls=%fused_computation | convolution fusion | flops 134488064 | bytes 3145728 | tf_op jit(solution)/shard_map/dot_general | solution.py:40
  136.3 3.1 %fusion = bf16[4096,64]{0,1:T(8,128)(2,1)} fusion(bf16[128,4096]{1,0:T(8,128)(2,1)S(1)} %bitcast.295, bf16[128,4096]{1,0:T(8,128)(2,1)} %reshape.691, bf16[64,4096]{1,0:T(8,128)(2,1)} %param.15), kind=kOutput, calls=%fused_computation.2 | convolution fusion | flops 134488064 | bytes 3145728 | tf_op jit(solution)/shard_map/dot_general | solution.py:40
  139.4 2.3 pad_maximum_fusion.1
  141.7 1.5 convolution_bitcast_fusion.1
  149.5 0.9 copy.73
  150.4 4.2 %all-to-all-start.5 = ((bf16[2,512,1,128]{3,0,2,1:T(2,128)(2,1)}), bf16[2,512,1,128]{3,0,2,1:T(2,128)(2,1)S(1)}, u32[]{:S(2)}, u32[]{:S(2)}) async-start(bf16[2,512,1,128]{3,0,2,1:T(2,128)(2,1)} %copy.73), calls=%async_computation.5 | async-start | bytes 524288 | tf_op jit(solution)/shard_map/all_to_all | solution.py:245
  154.6 24.8 %reduce-scatter.2.cloned.1.call-done = bf16[512,128]{0,1:T(8,128)(2,1)} async-done(((bf16[4096,128]{0,1:T(8,128)(2,1)}), bf16[512,128]{0,1:T(8,128)(2,1)}) %reduce-scatter.2.cloned.1.call-update) | async-done | bytes 131088 | tf_op jit(solution)/shard_map/reduce_scatter | solution.py:261
  179.4 1.5 slice_bitcast_fusion.32
  181.2 0.8 reshape_transpose_reshape.15
  182.3 0.8 reshape_transpose_reshape.14
  183.1 1.6 reshape_reshape.3
  184.7 32.4 %all-reduce.3.cloned.1.call-done = (bf16[512,64]{0,1:T(8,128)(2,1)}, bf16[64,512]{1,0:T(8,128)(2,1)}) async-done(((bf16[512,64]{0,1:T(8,128)(2,1)}, bf16[64,512]{1,0:T(8,128)(2,1)}), (bf16[512,64]{0,1:T(8,128)(2,1)}, bf16[64,512]{1,0:T(8,128)(2,1)})) %all-reduce.3.cloned.1.call-update) | async-done | bytes 131088 | tf_op jit(solution)/shard_map/psum | solution.py:276
  217.1 1.5 convert_element_type.317
  218.6 1.5 transpose.52
  (152 shorter events, 26.7 us)
Async XLA Ops:
  7.2 126.0 %copy-start = (bf16[2,64,4096]{2,1,0:T(8,128)(2,1)S(1)}, bf16[2,64,4096]{2,1,0:T(8,128)(2,1)}, u32[]{:S(2)}) copy-start(bf16[2,64,4096]{2,1,0:T(8,128)(2,1)} %param.13) | copy-start | bytes 3145732
  9.0 18.5 %all-to-all-start.1 = ((bf16[2,64,8,128]{3,1,0,2:T(8,128)(2,1)}), bf16[2,64,8,128]{3,1,0,2:T(8,128)(2,1)S(1)}, u32[]{:S(2)}, u32[]{:S(2)}) async-start(bf16[2,64,8,128]{3,1,0,2:T(8,128)(2,1)} %copy_bitcast_fusion.2), calls=%async_computation.1 | async-start | bytes 524288 | tf_op jit(solution)/shard_map/all_to_all | solution.py:182
  18.6 6.9 %copy-start.30 = (bf16[2,64,4096]{2,1,0:T(8,128)(2,1)S(1)}, bf16[2,64,4096]{2,1,0:T(8,128)(2,1)}, u32[]{:S(2)}) copy-start(bf16[2,64,4096]{2,1,0:T(8,128)(2,1)} %param.12) | copy-start | bytes 3145732
  19.6 25.0 %copy-start.25 = (f32[512,64]{1,0:T(8,128)}, f32[512,64]{1,0:T(8,128)S(1)}, u32[]{:S(2)}) copy-start(f32[512,64]{1,0:T(8,128)S(1)} %get-tuple-element.99) | copy-start | bytes 393220
  19.6 25.0 %copy-start.27 = (f32[512,64]{1,0:T(8,128)}, f32[512,64]{1,0:T(8,128)S(1)}, u32[]{:S(2)}) copy-start(f32[512,64]{1,0:T(8,128)S(1)} %get-tuple-element.100) | copy-start | bytes 393220
  27.5 11.1 %all-to-all-start.3 = ((bf16[2,64,8,128]{3,1,0,2:T(8,128)(2,1)}), bf16[2,64,8,128]{3,1,0,2:T(8,128)(2,1)S(1)}, u32[]{:S(2)}, u32[]{:S(2)}) async-start(bf16[2,64,8,128]{3,1,0,2:T(8,128)(2,1)} %copy_bitcast_fusion.1), calls=%async_computation.3 | async-start | bytes 524288 | tf_op jit(solution)/shard_map/all_to_all | solution.py:183
  38.6 0.7 copy-start.31
  39.3 18.9 %all-to-all-start = ((bf16[8,2,64,4,128]{4,3,2,1,0:T(4,128)(2,1)}), bf16[8,2,64,4,128]{4,3,2,1,0:T(4,128)(2,1)S(1)}, u32[]{:S(2)}, u32[]{:S(2)}) async-start(bf16[8,2,64,4,128]{4,3,2,1,0:T(4,128)(2,1)} %fusion.50), calls=%async_computation | async-start | bytes 2097152 | tf_op jit(solution)/shard_map/all_to_all | solution.py:177
  58.2 1.0 copy-start.24
  59.2 19.6 %all-to-all-start.2 = ((bf16[2,64,32,128]{3,1,0,2:T(8,128)(2,1)}), bf16[2,64,32,128]{3,1,0,2:T(8,128)(2,1)}, u32[]{:S(2)}, u32[]{:S(2)}) async-start(bf16[2,64,32,128]{3,1,0,2:T(8,128)(2,1)} %copy_bitcast_fusion), calls=%async_computation.2 | async-start | bytes 2097152 | tf_op jit(solution)/shard_map/all_to_all | solution.py:184
  65.0 1.0 copy-start.26
  65.1 1.0 copy-start.28
  78.8 1.6 copy-start.35
  80.2 0.9 copy-start.34
  80.4 15.6 %copy-start.29 = (bf16[2,512,4,128]{3,1,2,0:T(8,128)(2,1)}, bf16[2,512,4,128]{3,1,2,0:T(8,128)(2,1)S(1)}, u32[]{:S(2)}) copy-start(bf16[2,512,4,128]{3,1,2,0:T(8,128)(2,1)S(1)} %bitcast_select_fusion) | copy-start | bytes 3145732
  83.7 1.2 copy-start.2
  83.7 1.6 copy-start.22
  83.7 1.9 copy-start.23
  91.6 1.2 copy-start.4
  91.6 1.2 copy-start.7
  91.6 1.2 copy-start.9
  92.2 1.2 copy-start.1
  92.2 1.5 copy-start.19
  92.2 2.0 copy-start.21
  92.9 1.9 copy-start.6
  96.0 0.8 copy-start.41
  96.0 2.3 %copy-start.43 = (f32[512]{0:T(512)}, f32[512]{0:T(512)S(1)}, u32[]{:S(2)}) copy-start(f32[512]{0:T(512)S(1)} %get-tuple-element.10) | copy-start | bytes 6148
  97.8 0.9 copy-start.13
  97.8 1.0 copy-start.15
  97.8 1.3 copy-start.11
  98.8 1.9 copy-start.17
  101.9 6.7 %copy-start.44 = (f32[512]{0:T(512)S(1)}, f32[512]{0:T(512)}, u32[]{:S(2)}) copy-start(f32[512]{0:T(512)} %copy-done.43) | copy-start | bytes 6148
  104.3 19.6 %all-to-all-start.4 = ((bf16[2,512,4,128]{3,2,0,1:T(4,128)(2,1)}), bf16[2,512,4,128]{3,2,0,1:T(4,128)(2,1)}, u32[]{:S(2)}, u32[]{:S(2)}) async-start(bf16[2,512,4,128]{3,2,0,1:T(4,128)(2,1)} %copy.70), calls=%async_computation.4 | async-start | bytes 2097152 | tf_op jit(solution)/shard_map/all_to_all | solution.py:244
  108.6 1.7 copy-start.20
  108.6 1.7 copy-start.42
  110.3 1.4 copy-start.36
  110.3 1.4 copy-start.37
  110.3 1.4 copy-start.38
  110.3 1.4 copy-start.39
  110.3 1.4 copy-start.40
  111.8 1.3 copy-start.10
  111.9 2.2 copy-start.8
  123.9 26.4 %all-to-all-start.6 = ((bf16[2,512,1,128]{3,0,2,1:T(2,128)(2,1)}), bf16[2,512,1,128]{3,0,2,1:T(2,128)(2,1)S(1)}, u32[]{:S(2)}, u32[]{:S(2)}) async-start(bf16[2,512,1,128]{3,0,2,1:T(2,128)(2,1)} %copy.76), calls=%async_computation.6 | async-start | bytes 524288 | tf_op jit(solution)/shard_map/all_to_all | solution.py:246
  127.4 52.1 %reduce-scatter.2.cloned.1.call-start = ((), (), s32[]{:S(2)}) async-start(), calls=%async_computation.8 | async-start | bytes 1179648 | tf_op jit(solution)/shard_map/reduce_scatter | solution.py:261
  141.7 1.5 copy-start.16
  143.2 1.0 copy-start.14
  144.3 1.0 copy-start.12
  145.3 1.0 copy-start.18
  146.4 1.0 copy-start.5
  146.4 1.4 copy-start.33
  146.4 2.0 copy-start.32
  150.4 32.7 %copy-start.3 = (bf16[2,64,8,4,128]{4,3,2,1,0:T(4,128)(2,1)S(1)}, bf16[2,64,8,4,128]{4,3,2,1,0:T(4,128)(2,1)}, u32[]{:S(2)}) copy-start(bf16[2,64,8,4,128]{4,3,2,1,0:T(4,128)(2,1)} %copy.72) | copy-start | bytes 3145732
  150.4 31.7 %all-to-all-start.5 = ((bf16[2,512,1,128]{3,0,2,1:T(2,128)(2,1)}), bf16[2,512,1,128]{3,0,2,1:T(2,128)(2,1)S(1)}, u32[]{:S(2)}, u32[]{:S(2)}) async-start(bf16[2,512,1,128]{3,0,2,1:T(2,128)(2,1)} %copy.73), calls=%async_computation.5 | async-start | bytes 524288 | tf_op jit(solution)/shard_map/all_to_all | solution.py:245
  154.6 62.5 %all-reduce.3.cloned.1.call-start = ((), (), s32[]{:S(2)}) async-start(), calls=%async_computation.9 | async-start | bytes 262144 | tf_op jit(solution)/shard_map/psum | solution.py:276
Sparse Core Ops, SparseCore 0:
  141.8 37.5 reduce-scatter.1
  182.4 34.6 all-reduce.2
